TPU v7x, 128 devices: a whole 4x4x4 slice. The times are simulated.
128 devices in a mesh: dp: 16 (over y, x), expert: 4 (over z), tensor: 2 (over core).
Axes of the slice: x: 4, y: 4, z: 4, core: 2. Of those that a mesh axis runs over, the one named last changes fastest.
Arguments:
- tokens: bfloat16 [8192, 2048], P(('dp', 'expert'), 'tensor'), may hold values from -6 to 6
- norm_gain: bfloat16 [2048], replicated, may hold values from 0.25 to 1.75
- expert_ids: int32 [8192, 2], P(('dp', 'expert')), may hold values from 0 to 3, all different within a row; in each aligned block of 128 rows (0 to 127, 128 to 255, ...) at most 128 rows name the same one
- gate_codes: int32 [8192, 2], P(('dp', 'expert')), may hold values from 1 to 255
- gate_weights: bfloat16 [4, 7168, 2048], P('expert', ('dp', 'tensor')), may hold values from -0.125 to 0.125
- up_weights: bfloat16 [4, 7168, 2048], P('expert', ('dp', 'tensor')), may hold values from -0.125 to 0.125
- down_weights: bfloat16 [4, 7168, 2048], P('expert', ('dp', 'tensor')), may hold values from -0.0625 to 0.0625
- value_head: bfloat16 [2048, 128], replicated, may hold values from -0.125 to 0.125
- actions: int32 [8192], P(('dp', 'expert')), may hold values from 0 to 127
- rewards: int32 [8192], P(('dp', 'expert')), may hold values from -8 to 8
- trace_codes: int32 [8192], P(('dp', 'expert')), may hold values from 1 to 1024
Outputs:
- action_values: float32 [8192, 128], P(('dp', 'expert'))
- retrace_targets: float32 [8192], P(('dp', 'expert'))
Inputs may be any that keep to these rules, and one draw needn't show every extreme that they name: `expert_ids`: each row names 2 different experts; within the 128 rows of one index pair of dp and expert each expert is named by at most 128 rows, and in some of these blocks one expert by exactly 128.
All inputs are finite; a program needn't handle non-finite values.
Results may differ from a plain program's by a relative error of at most 0.005.
Values may be sent and summed in bfloat16 or wider, within the bound.
A program may use at most 256 MiB of HBM per device.

v0:
```python
import jax
import jax.numpy as jnp
from jax import lax
from jax.sharding import PartitionSpec as P

STEPS = 128
DISCOUNT = 0.99
EPSILON = 1e-05
HIGHEST = lax.Precision.HIGHEST


def retrace(action_values, actions, rewards, trace_codes):
    greedy = jnp.max(action_values, axis=1)
    picked = (
        actions[:, None] == jnp.arange(action_values.shape[1], dtype=jnp.int32)[None, :]
    ).astype(jnp.float32)
    taken = jnp.sum(action_values * picked, axis=1)
    trace = trace_codes.astype(jnp.float32) / 1024.0
    reward = rewards.astype(jnp.float32) * 0.25
    greedy = greedy.reshape(-1, STEPS)
    taken = taken.reshape(-1, STEPS)
    trace = trace.reshape(-1, STEPS)
    reward = reward.reshape(-1, STEPS)
    padding = jnp.zeros_like(greedy[:, :1])
    greedy_next = jnp.concatenate([greedy[:, 1:], padding], axis=1)
    taken_next = jnp.concatenate([taken[:, 1:], padding], axis=1)
    trace_next = jnp.concatenate([trace[:, 1:], padding], axis=1)
    driver = reward + DISCOUNT * (greedy_next - trace_next * taken_next)
    log_sums = jnp.cumsum(jnp.log(DISCOUNT * trace), axis=1)
    spans = log_sums[:, None, :] - log_sums[:, :, None]
    upper_mask = (
        jnp.arange(STEPS, dtype=jnp.int32)[None, :] >= jnp.arange(STEPS, dtype=jnp.int32)[:, None]
    )
    weight = jnp.where(upper_mask[None, :, :], jnp.exp(jnp.minimum(spans, 0.0)), 0.0)
    target = jnp.einsum("nts,ns->nt", weight, driver, precision=HIGHEST)
    return target.reshape(-1)


def rows_by(a, b):
    return lax.dot_general(a, b, (((1,), (1,)), ((), ())), preferred_element_type=jnp.float32)


def per_device(
    tokens,
    norm_gain,
    expert_ids,
    gate_codes,
    gate_weights,
    up_weights,
    down_weights,
    value_head,
    actions,
    rewards,
    trace_codes,
):
    dp, ex = (lax.axis_size("dp"), lax.axis_size("expert"))
    tp = lax.axis_size("tensor")
    rows, half = tokens.shape
    folded = jnp.dot(down_weights[0], value_head, preferred_element_type=jnp.float32)
    folded = folded.astype(jnp.bfloat16)
    wide = tokens.astype(jnp.float32)
    square = lax.psum(jnp.sum(wide * wide, axis=1, keepdims=True), "tensor") / (half * tp)
    gain = lax.dynamic_slice_in_dim(norm_gain, lax.axis_index("tensor") * half, half)
    normed = wide * lax.rsqrt(square + EPSILON) * gain.astype(jnp.float32)[None, :]
    normed = normed.astype(jnp.bfloat16)
    everyone = lax.all_gather(normed, ("dp", "expert", "tensor"), axis=0)
    everyone = everyone.reshape(dp * ex, tp, rows, half)
    left = everyone[:, 0].reshape(dp * ex * rows, half)
    right = everyone[:, 1].reshape(dp * ex * rows, half)
    gate_m, up_m = (gate_weights[0], up_weights[0])
    gate = rows_by(left, gate_m[:, :half]) + rows_by(right, gate_m[:, half:])
    lift = rows_by(left, up_m[:, :half]) + rows_by(right, up_m[:, half:])
    hidden = (jax.nn.silu(gate) * lift).astype(jnp.bfloat16)
    value = jnp.dot(hidden, folded, preferred_element_type=jnp.float32)
    value = lax.psum_scatter(value, "dp", scatter_dimension=0, tiled=True)
    value = value.reshape(ex, rows, value.shape[1])
    value = lax.all_to_all(value, "expert", split_axis=0, concat_axis=0, tiled=True)
    codes = gate_codes.astype(jnp.float32)
    share = codes / jnp.sum(codes, axis=1, keepdims=True)
    named = expert_ids[None] == jnp.arange(ex, dtype=jnp.int32)[:, None, None]
    by_expert = jnp.sum(jnp.where(named, share[None], 0.0), axis=2)
    blended = jnp.sum(value * by_expert[:, :, None], axis=0)
    action_values = lax.psum(blended, "tensor")
    return (action_values, retrace(action_values, actions, rewards, trace_codes))


def solution(mesh):
    group, weight = (P(("dp", "expert"), None), P("expert", ("dp", "tensor"), None))
    line = P(("dp", "expert"))
    in_specs = (
        P(("dp", "expert"), "tensor"),
        P(),
        group,
        group,
        weight,
        weight,
        weight,
        P(),
        line,
        line,
        line,
    )
    return jax.shard_map(
        per_device, mesh=mesh, in_specs=in_specs, out_specs=(group, line), check_vma=False
    )
```

profile of v0, /device:TPU:1, one launch (start us, length us, event | category | flops | bytes accessed | tf_op | source)
XLA Modules:
  0.0 304.3 jit_solution(3037245187421249182)
XLA Ops:
  7.2 0.0 copy-start
  7.2 0.0 all-gather.3.cloned.1.call-start
  7.2 1.2 fusion.4
  8.4 3.5 %psum.14 = f32[128,1]{0,1:T(1,128)S(1)} all-reduce(f32[128,1]{0,1:T(1,128)S(1)} %bitcast.47), channel_id=1, replica_groups=mesh['dp'=16,'expert'=4,'tensor'=2] {'tensor'}, use_global_device_ids=true, to_apply=%region_1.0 | all-reduce | flops 128 | bytes 1024 | tf_op jit(solution)/shard_map/psum | solution.py:62
  11.9 0.7 dynamic-slice_convert_fusion
  12.6 1.8 fusion.6
  14.4 0.0 all-gather.3.cloned.1.call-update
  14.4 0.0 reduce-scatter.2.cloned.1.call-start
  14.4 0.0 copy-done
  14.4 1.4 convolution_convert_fusion
  15.9 107.5 %all-gather.3.cloned.1.call-done = bf16[16384,1024]{1,0:T(8,128)(2,1)} async-done(((bf16[128,1024]{1,0:T(8,128)(2,1)}), bf16[16384,1024]{1,0:T(8,128)(2,1)}) %all-gather.3.cloned.1.call-update) | async-done | bytes 33554448 | tf_op jit(solution)/shard_map/all_gather | solution.py:66
  123.4 0.0 copy-start.2
  123.4 18.8 %fusion.36 = (bf16[64,1,128,1024]{3,2,1,0:T(8,128)(2,1)}, bf16[64,1,128,1024]{3,2,1,0:T(8,128)(2,1)S(1)}) fusion(bf16[64,2,128,1024]{3,2,1,0:T(8,128)(2,1)} %bitcast.39), kind=kLoop, calls=%fused_computation.58 | loop fusion | bytes 67108864 | tf_op jit(solution)/shard_map/slice | solution.py:69
  142.2 0.0 copy-done.2
  142.2 0.0 copy-start.3
  142.2 5.0 %fusion.12 = f32[8192,224]{0,1:T(8,128)S(1)} fusion(bf16[8192,1024]{1,0:T(8,128)(2,1)S(1)} %bitcast.35, bf16[224,2048]{1,0:T(8,128)(2,1)S(1)} %bitcast.40), kind=kOutput, calls=%fused_computation.17 | convolution fusion | flops 3758096384 | bytes 24576000 | tf_op jit(solution)/shard_map/dot_general | solution.py:40
  147.3 0.0 copy-done.3
  147.3 7.2 %fusion.9 = f32[8192,224]{0,1:T(8,128)} fusion(bf16[8192,1024]{1,0:T(8,128)(2,1)S(1)} %bitcast.36, bf16[224,2048]{1,0:T(8,128)(2,1)S(1)} %bitcast.43), kind=kOutput, calls=%fused_computation.14 | convolution fusion | flops 3758096384 | bytes 24576000 | tf_op jit(solution)/shard_map/dot_general | solution.py:40
  154.5 13.9 %convolution_add_fusion.1 = f32[8192,224]{0,1:T(8,128)} fusion(f32[8192,224]{0,1:T(8,128)S(1)} %fusion.12, bf16[8192,1024]{1,0:T(8,128)(2,1)} %bitcast.37, bf16[224,2048]{1,0:T(8,128)(2,1)S(1)} %bitcast.41), kind=kOutput, calls=%fused_computation.2 | convolution fusion | flops 3759931392 | bytes 31916032 | tf_op jit(solution)/shard_map/dot_general | solution.py:40
  168.4 0.0 copy-start.4
  168.4 0.0 copy-start.5
  168.4 0.0 copy-start.7
  168.4 0.0 copy-start.6
  168.4 0.0 copy-start.8
  168.4 0.0 copy-start.1
  168.5 15.5 %fusion.2 = f32[8192,128]{1,0:T(8,128)} fusion(bf16[224,128]{1,0:T(8,128)(2,1)S(1)} %convolution_convert_fusion, f32[8192,224]{0,1:T(8,128)} %fusion.9, bf16[8192,1024]{1,0:T(8,128)(2,1)} %bitcast.38, f32[8192,224]{0,1:T(8,128)} %convolution_add_fusion.1, bf16[224,2048]{1,0:T(8,128)(2,1)S(1)} %bitcast.44), kind=kOutput, calls=%fused_computation.4 | convolution fusion | flops 4240703488 | bytes 36167680 | tf_op jit(solution)/shard_map/dot_general | solution.py:74
  183.9 0.0 reduce-scatter.2.cloned.1.call-update
  183.9 0.0 copy-done.4
  184.0 0.0 copy-done.5
  184.0 75.6 %reduce-scatter.2.cloned.1.call-done = f32[512,128]{1,0:T(8,128)} async-done(((f32[8192,128]{1,0:T(8,128)}), f32[512,128]{1,0:T(8,128)}) %reduce-scatter.2.cloned.1.call-update) | async-done | bytes 262160 | tf_op jit(solution)/shard_map/reduce_scatter | solution.py:75
  259.6 4.1 %all-to-all-start = ((f32[4,128,128]{2,1,0:T(8,128)}), f32[4,128,128]{2,1,0:T(8,128)S(1)}, u32[]{:S(2)}, u32[]{:S(2)}) async-start(f32[4,128,128]{2,1,0:T(8,128)} %bitcast.42), calls=%async_computation.1 | async-start | bytes 524288 | tf_op jit(solution)/shard_map/all_to_all | solution.py:77
  263.7 0.0 all-reduce.2.cloned.1.call-start
  263.7 0.0 copy-done.7
  263.7 5.5 %all-to-all-done = f32[4,128,128]{2,1,0:T(8,128)S(1)} async-done(((f32[4,128,128]{2,1,0:T(8,128)}), f32[4,128,128]{2,1,0:T(8,128)S(1)}, u32[]{:S(2)}, u32[]{:S(2)}) %all-to-all-start) | async-done | bytes 262176 | tf_op jit(solution)/shard_map/all_to_all | solution.py:77
  269.2 0.8 multiply_reduce_fusion
  270.0 0.0 all-reduce.2.cloned.1.call-update
  270.0 0.1 slice_bitcast_fusion.1
  270.1 0.1 copy.19
  270.2 0.2 reduce-window.7
  270.4 0.1 reduce
  270.5 23.9 %all-reduce.2.cloned.1.call-done = f32[128,128]{1,0:T(8,128)} async-done(((f32[128,128]{1,0:T(8,128)}), f32[128,128]{1,0:T(8,128)}) %all-reduce.2.cloned.1.call-update) | async-done | bytes 65552 | tf_op jit(solution)/shard_map/psum | solution.py:83
  294.4 0.0 copy-done.6
  294.4 1.0 select_reduce_fusion
  295.4 0.1 slice_bitcast_fusion
  295.5 0.0 copy-done.8
  295.5 0.8 convolution_bitcast_fusion
  296.3 1.5 copy.21
  297.8 0.0 copy-done.1
  (5 shorter events, 0.1 us)
Async XLA Ops:
  7.2 7.3 %copy-start = (bf16[1,224,2048]{2,1,0:T(8,128)(2,1)S(1)}, bf16[1,224,2048]{2,1,0:T(8,128)(2,1)}, u32[]{:S(2)}) copy-start(bf16[1,224,2048]{2,1,0:T(8,128)(2,1)} %param.17) | copy-start | bytes 2752516
  7.2 116.3 %all-gather.3.cloned.1.call-start = ((), (), s32[]{:S(2)}) async-start(), calls=%async_computation.4 | async-start | bytes 33816576 | tf_op jit(solution)/shard_map/all_gather | solution.py:66
  14.4 245.2 %reduce-scatter.2.cloned.1.call-start = ((), (), s32[]{:S(2)}) async-start(), calls=%async_computation.2 | async-start | bytes 4456448 | tf_op jit(solution)/shard_map/reduce_scatter | solution.py:75
  123.4 18.8 %copy-start.2 = (bf16[1,224,2048]{2,1,0:T(8,128)(2,1)S(1)}, bf16[1,224,2048]{2,1,0:T(8,128)(2,1)}, u32[]{:S(2)}) copy-start(bf16[1,224,2048]{2,1,0:T(8,128)(2,1)} %param.15) | copy-start | bytes 2752516
  142.2 5.1 %copy-start.3 = (bf16[1,224,2048]{2,1,0:T(8,128)(2,1)S(1)}, bf16[1,224,2048]{2,1,0:T(8,128)(2,1)}, u32[]{:S(2)}) copy-start(bf16[1,224,2048]{2,1,0:T(8,128)(2,1)} %param.16) | copy-start | bytes 2752516
  168.4 15.5 %copy-start.4 = (s32[128,2]{0,1:T(2,128)S(1)}, s32[128,2]{0,1:T(2,128)}, u32[]{:S(2)}) copy-start(s32[128,2]{0,1:T(2,128)} %param.14) | copy-start | bytes 3076
  168.4 15.6 %copy-start.5 = (s32[128,2]{0,1:T(2,128)S(1)}, s32[128,2]{0,1:T(2,128)}, u32[]{:S(2)}) copy-start(s32[128,2]{0,1:T(2,128)} %param.13) | copy-start | bytes 3076
  168.4 95.3 %copy-start.7 = (s32[128]{0:T(128)S(1)}, s32[128]{0:T(128)}, u32[]{:S(2)}) copy-start(s32[128]{0:T(128)} %param.21) | copy-start | bytes 1540
  168.4 126.0 %copy-start.6 = (s32[128]{0:T(128)S(1)}, s32[128]{0:T(128)}, u32[]{:S(2)}) copy-start(s32[128]{0:T(128)} %param.19) | copy-start | bytes 1540
  168.4 127.0 %copy-start.8 = (s32[128]{0:T(128)S(1)}, s32[128]{0:T(128)}, u32[]{:S(2)}) copy-start(s32[128]{0:T(128)} %param.20) | copy-start | bytes 1540
  168.4 129.3 %copy-start.1 = (bf16[1,224,2048]{2,1,0:T(8,128)(2,1)S(1)}, bf16[1,224,2048]{2,1,0:T(8,128)(2,1)}, u32[]{:S(2)}) copy-start(bf16[1,224,2048]{2,1,0:T(8,128)(2,1)} %param.17) | copy-start | bytes 2752516
  259.6 9.7 %all-to-all-start = ((f32[4,128,128]{2,1,0:T(8,128)}), f32[4,128,128]{2,1,0:T(8,128)S(1)}, u32[]{:S(2)}, u32[]{:S(2)}) async-start(f32[4,128,128]{2,1,0:T(8,128)} %bitcast.42), calls=%async_computation.1 | async-start | bytes 524288 | tf_op jit(solution)/shard_map/all_to_all | solution.py:77
  263.7 30.7 %all-reduce.2.cloned.1.call-start = ((), (), s32[]{:S(2)}) async-start(), calls=%async_computation.3 | async-start | bytes 131072 | tf_op jit(solution)/shard_map/psum | solution.py:83
Sparse Core Ops, SparseCore 0:
  14.5 108.8 all-gather.2
  184.1 75.4 reduce-scatter.1
  270.1 24.1 all-reduce.1
where the time goes:
time: 305 us; the launch traced here: 304 us
  waiting for transfers between devices  213 us (70%)
  matrix products  43.9 us (14%)
  local copies, waits for them, and re-layouts  20.6 us (7%)
  between operations  13.8 us (5%)
  other arithmetic  5.72 us (2%)
  starting transfers between devices  4.22 us (1%)
  blocking collectives  3.5 us (1%)
    all_gather x1, waiting for transfers between devices, per_device(): everyone = lax.all_gather(normed, ('dp', 'expert', 'tensor'), axis=0)  108 us
    reduce_scatter x1, waiting for transfers between devices, per_device(): value = lax.psum_scatter(value, 'dp', scatter_dimension=0, tiled=True)  75.6 us
    dot_general x3, matrix products, rows_by(): lax.dot_general(a, b, (((1,), (1,)), ((), ())), preferred_element_type=jn...  26.2 us
    psum x1, waiting for transfers between devices, per_device(): action_values = lax.psum(blended, 'tensor')  23.9 us
    slice x1, local copies, waits for them, and re-layouts, per_device(): right = everyone[:, 1].reshape(dp * ex * rows, half)  18.8 us
    dot_general x1, matrix products, per_device(): value = jnp.dot(hidden, folded, preferred_element_type=jnp.float32)  15.5 us
  transfers between devices with their start and end apart: 4, of which 4 were waited for; matrix products, arithmetic and copies ran while one was open for 1% of the time, Pallas kernels for 0%

commit v1 on v0

--- a/solution.py
+++ b/solution.py
@@ -7,6 +7,12 @@
 DISCOUNT = 0.99
 EPSILON = 1e-05
 HIGHEST = lax.Precision.HIGHEST
+
+
+def add_all(x, axis):
+    pieces = lax.all_gather(x, axis, axis=0, tiled=False)
+    result = pieces.sum(axis=0)
+    return result
 
 
 def retrace(action_values, actions, rewards, trace_codes):
@@ -80,7 +86,7 @@
     named = expert_ids[None] == jnp.arange(ex, dtype=jnp.int32)[:, None, None]
     by_expert = jnp.sum(jnp.where(named, share[None], 0.0), axis=2)
     blended = jnp.sum(value * by_expert[:, :, None], axis=0)
-    action_values = lax.psum(blended, "tensor")
+    action_values = add_all(blended, "tensor")
     return (action_values, retrace(action_values, actions, rewards, trace_codes))
 
 

time: 305 us -> 283 us (0.928)
  waiting for transfers between devices: 213 us -> 188 us
  blocking collectives: 3.5 us -> 8.93 us
    psum x1 -> x0, waiting for transfers between devices: 23.9 us -> none  [per_device(): action_values = lax.psum(blended, 'tensor')]
    all_gather x0 -> x1, blocking collectives: none -> 5.42 us  [add_all(): pieces = lax.all_gather(x, axis, axis=0, tiled=False)]
  transfers between devices with their start and end apart: 4 -> 3, of which waited for: 4 -> 3; matrix products, arithmetic and copies ran while one was open for 1% -> 1% of each run, Pallas kernels for 0% -> 0%
where the time goes in v1:
time: 283 us
  waiting for transfers between devices  188 us (66%)
  matrix products  43.9 us (16%)
  local copies, waits for them, and re-layouts  19.1 us (7%)
  between operations  14.2 us (5%)
  blocking collectives  8.93 us (3%)
  other arithmetic  4.27 us (2%)
  starting transfers between devices  4.22 us (1%)
    all_gather x1, waiting for transfers between devices, per_device(): everyone = lax.all_gather(normed, ('dp', 'expert', 'tensor'), axis=0)  108 us
    reduce_scatter x1, waiting for transfers between devices, per_device(): value = lax.psum_scatter(value, 'dp', scatter_dimension=0, tiled=True)  75.2 us
    dot_general x3, matrix products, rows_by(): lax.dot_general(a, b, (((1,), (1,)), ((), ())), preferred_element_type=jn...  26.2 us
    slice x1, local copies, waits for them, and re-layouts, per_device(): right = everyone[:, 1].reshape(dp * ex * rows, half)  18.8 us
    dot_general x1, matrix products, per_device(): value = jnp.dot(hidden, folded, preferred_element_type=jnp.float32)  15.5 us
  transfers between devices with their start and end apart: 3, of which 3 were waited for; matrix products, arithmetic and copies ran while one was open for 1% of the time, Pallas kernels for 0%

profile of v1, /device:TPU:1, one launch (start us, length us, event | category | flops | bytes accessed | tf_op | source)
XLA Modules:
  0.0 282.8 jit_solution(2341151903078865495)
XLA Ops:
  7.2 0.0 copy-start
  7.2 0.0 all-gather.4.cloned.1.call-start
  7.2 1.2 fusion.4
  8.4 3.5 %psum.7 = f32[128,1]{0,1:T(1,128)S(1)} all-reduce(f32[128,1]{0,1:T(1,128)S(1)} %bitcast.49), channel_id=1, replica_groups=mesh['dp'=16,'expert'=4,'tensor'=2] {'tensor'}, use_global_device_ids=true, to_apply=%region_1.0 | all-reduce | flops 128 | bytes 1024 | tf_op jit(solution)/shard_map/psum | solution.py:68
  11.9 0.7 dynamic-slice_convert_fusion
  12.6 1.8 fusion.6
  14.4 0.0 all-gather.4.cloned.1.call-update
  14.4 0.0 reduce-scatter.2.cloned.1.call-start
  14.4 0.0 copy-done
  14.4 1.4 convolution_convert_fusion
  15.9 107.5 %all-gather.4.cloned.1.call-done = bf16[16384,1024]{1,0:T(8,128)(2,1)} async-done(((bf16[128,1024]{1,0:T(8,128)(2,1)}), bf16[16384,1024]{1,0:T(8,128)(2,1)}) %all-gather.4.cloned.1.call-update) | async-done | bytes 33554448 | tf_op jit(solution)/shard_map/all_gather | solution.py:72
  123.4 0.0 copy-start.2
  123.4 18.8 %fusion.36 = (bf16[64,1,128,1024]{3,2,1,0:T(8,128)(2,1)}, bf16[64,1,128,1024]{3,2,1,0:T(8,128)(2,1)S(1)}) fusion(bf16[64,2,128,1024]{3,2,1,0:T(8,128)(2,1)} %bitcast.40), kind=kLoop, calls=%fused_computation.58 | loop fusion | bytes 67108864 | tf_op jit(solution)/shard_map/slice | solution.py:75
  142.2 0.0 copy-done.2
  142.2 0.0 copy-start.4
  142.2 5.0 %fusion.12 = f32[8192,224]{0,1:T(8,128)S(1)} fusion(bf16[8192,1024]{1,0:T(8,128)(2,1)S(1)} %bitcast.36, bf16[224,2048]{1,0:T(8,128)(2,1)S(1)} %bitcast.41), kind=kOutput, calls=%fused_computation.17 | convolution fusion | flops 3758096384 | bytes 24576000 | tf_op jit(solution)/shard_map/dot_general | solution.py:46
  147.3 0.0 copy-done.4
  147.3 7.2 %fusion.9 = f32[8192,224]{0,1:T(8,128)} fusion(bf16[8192,1024]{1,0:T(8,128)(2,1)S(1)} %bitcast.37, bf16[224,2048]{1,0:T(8,128)(2,1)S(1)} %bitcast.45), kind=kOutput, calls=%fused_computation.14 | convolution fusion | flops 3758096384 | bytes 24576000 | tf_op jit(solution)/shard_map/dot_general | solution.py:46
  154.5 13.9 %convolution_add_fusion.1 = f32[8192,224]{0,1:T(8,128)} fusion(f32[8192,224]{0,1:T(8,128)S(1)} %fusion.12, bf16[8192,1024]{1,0:T(8,128)(2,1)} %bitcast.38, bf16[224,2048]{1,0:T(8,128)(2,1)S(1)} %bitcast.42), kind=kOutput, calls=%fused_computation.2 | convolution fusion | flops 3759931392 | bytes 31916032 | tf_op jit(solution)/shard_map/dot_general | solution.py:46
  168.4 0.0 copy-start.8
  168.4 0.0 copy-start.5
  168.4 0.0 copy-start.6
  168.4 0.0 copy-start.7
  168.4 0.0 copy-start.9
  168.4 0.0 copy-start.1
  168.5 15.5 %fusion.2 = f32[8192,128]{1,0:T(8,128)} fusion(bf16[224,128]{1,0:T(8,128)(2,1)S(1)} %convolution_convert_fusion, f32[8192,224]{0,1:T(8,128)} %fusion.9, bf16[8192,1024]{1,0:T(8,128)(2,1)} %bitcast.39, f32[8192,224]{0,1:T(8,128)} %convolution_add_fusion.1, bf16[224,2048]{1,0:T(8,128)(2,1)S(1)} %bitcast.46), kind=kOutput, calls=%fused_computation.4 | convolution fusion | flops 4240703488 | bytes 36167680 | tf_op jit(solution)/shard_map/dot_general | solution.py:80
  183.9 0.0 reduce-scatter.2.cloned.1.call-update
  183.9 0.0 copy-done.8
  184.0 0.1 copy.19
  184.1 0.2 reduce-window.7
  184.2 0.1 reduce
  184.4 0.0 copy-done.5
  184.4 0.0 copy-done.6
  184.4 75.2 %reduce-scatter.2.cloned.1.call-done = f32[512,128]{1,0:T(8,128)} async-done(((f32[8192,128]{1,0:T(8,128)}), f32[512,128]{1,0:T(8,128)}) %reduce-scatter.2.cloned.1.call-update) | async-done | bytes 262160 | tf_op jit(solution)/shard_map/reduce_scatter | solution.py:81
  259.6 4.1 %all-to-all-start = ((f32[4,128,128]{2,1,0:T(8,128)}), f32[4,128,128]{2,1,0:T(8,128)S(1)}, u32[]{:S(2)}, u32[]{:S(2)}) async-start(f32[4,128,128]{2,1,0:T(8,128)} %bitcast.44), calls=%async_computation.1 | async-start | bytes 524288 | tf_op jit(solution)/shard_map/all_to_all | solution.py:83
  263.7 0.1 slice_bitcast_fusion.1
  263.8 5.5 %all-to-all-done = f32[4,128,128]{2,1,0:T(8,128)S(1)} async-done(((f32[4,128,128]{2,1,0:T(8,128)}), f32[4,128,128]{2,1,0:T(8,128)S(1)}, u32[]{:S(2)}, u32[]{:S(2)}) %all-to-all-start) | async-done | bytes 262176 | tf_op jit(solution)/shard_map/all_to_all | solution.py:83
  269.2 0.1 multiply_reduce_fusion
  269.4 5.4 %all-gather.1 = f32[256,128]{1,0:T(8,128)S(1)} all-gather(f32[128,128]{1,0:T(8,128)S(1)} %multiply_reduce_fusion), channel_id=3, replica_groups=mesh['dp'=16,'expert'=4,'tensor'=2] {'tensor'}, dimensions={0}, use_global_device_ids=true | all-gather | bytes 196608 | tf_op jit(solution)/shard_map/all_gather | solution.py:13
  274.8 0.0 copy-done.7
  274.8 0.0 copy-start.3
  274.8 0.2 select_reduce_fusion
  275.0 0.1 slice_bitcast_fusion
  275.1 0.0 copy-done.9
  275.1 0.8 convolution_bitcast_fusion
  275.9 0.0 copy-done.3
  275.9 0.0 copy-done.1
  (6 shorter events, 0.1 us)
Async XLA Ops:
  7.2 7.3 %copy-start = (bf16[1,224,2048]{2,1,0:T(8,128)(2,1)S(1)}, bf16[1,224,2048]{2,1,0:T(8,128)(2,1)}, u32[]{:S(2)}) copy-start(bf16[1,224,2048]{2,1,0:T(8,128)(2,1)} %param.17) | copy-start | bytes 2752516
  7.2 116.3 %all-gather.4.cloned.1.call-start = ((), (), s32[]{:S(2)}) async-start(), calls=%async_computation.3 | async-start | bytes 33816576 | tf_op jit(solution)/shard_map/all_gather | solution.py:72
  14.4 245.2 %reduce-scatter.2.cloned.1.call-start = ((), (), s32[]{:S(2)}) async-start(), calls=%async_computation.2 | async-start | bytes 4456448 | tf_op jit(solution)/shard_map/reduce_scatter | solution.py:81
  123.4 18.8 %copy-start.2 = (bf16[1,224,2048]{2,1,0:T(8,128)(2,1)S(1)}, bf16[1,224,2048]{2,1,0:T(8,128)(2,1)}, u32[]{:S(2)}) copy-start(bf16[1,224,2048]{2,1,0:T(8,128)(2,1)} %param.15) | copy-start | bytes 2752516
  142.2 5.1 %copy-start.4 = (bf16[1,224,2048]{2,1,0:T(8,128)(2,1)S(1)}, bf16[1,224,2048]{2,1,0:T(8,128)(2,1)}, u32[]{:S(2)}) copy-start(bf16[1,224,2048]{2,1,0:T(8,128)(2,1)} %param.16) | copy-start | bytes 2752516
  168.4 15.5 %copy-start.8 = (s32[128]{0:T(128)S(1)}, s32[128]{0:T(128)}, u32[]{:S(2)}) copy-start(s32[128]{0:T(128)} %param.21) | copy-start | bytes 1540
  168.4 15.9 %copy-start.5 = (s32[128,2]{0,1:T(2,128)S(1)}, s32[128,2]{0,1:T(2,128)}, u32[]{:S(2)}) copy-start(s32[128,2]{0,1:T(2,128)} %param.14) | copy-start | bytes 3076
  168.4 16.0 %copy-start.6 = (s32[128,2]{0,1:T(2,128)S(1)}, s32[128,2]{0,1:T(2,128)}, u32[]{:S(2)}) copy-start(s32[128,2]{0,1:T(2,128)} %param.13) | copy-start | bytes 3076
  168.4 106.4 %copy-start.7 = (s32[128]{0:T(128)S(1)}, s32[128]{0:T(128)}, u32[]{:S(2)}) copy-start(s32[128]{0:T(128)} %param.19) | copy-start | bytes 1540
  168.4 106.7 %copy-start.9 = (s32[128]{0:T(128)S(1)}, s32[128]{0:T(128)}, u32[]{:S(2)}) copy-start(s32[128]{0:T(128)} %param.20) | copy-start | bytes 1540
  168.4 107.5 %copy-start.1 = (bf16[1,224,2048]{2,1,0:T(8,128)(2,1)S(1)}, bf16[1,224,2048]{2,1,0:T(8,128)(2,1)}, u32[]{:S(2)}) copy-start(bf16[1,224,2048]{2,1,0:T(8,128)(2,1)} %param.17) | copy-start | bytes 2752516
  259.6 9.7 %all-to-all-start = ((f32[4,128,128]{2,1,0:T(8,128)}), f32[4,128,128]{2,1,0:T(8,128)S(1)}, u32[]{:S(2)}, u32[]{:S(2)}) async-start(f32[4,128,128]{2,1,0:T(8,128)} %bitcast.44), calls=%async_computation.1 | async-start | bytes 524288 | tf_op jit(solution)/shard_map/all_to_all | solution.py:83
  274.8 1.1 copy-start.3
Sparse Core Ops, SparseCore 0:
  14.5 108.8 all-gather.3
  184.1 75.4 reduce-scatter.1
